TPU v7x, 32 devices: a whole 2x2x4 slice. The times are simulated.
32 devices in a mesh: dp: 8 (over z, x), mp: 4 (over y, core).
Axes of the slice: x: 2, y: 2, z: 4, core: 2. Of those that a mesh axis runs over, the one named last changes fastest.
Arguments:
- query_rows: bfloat16 [2048, 2048], P('dp', 'mp'), may hold values from -6 to 6
- key_rows: bfloat16 [2048, 512], P('dp', 'mp'), may hold values from -6 to 6
- value_matrix: bfloat16 [2048, 512], P('dp', 'mp'), may hold values from -6 to 6
- out_weight: bfloat16 [2048, 5120], P('mp', 'dp'), may hold values from -0.125 to 0.125
- out_grad: bfloat16 [2048, 5120], P('dp', 'mp'), may hold values from -6 to 6
- doc_lengths: int32 [8, 8], P('dp'), may hold values from 1 to 249, as said below
Outputs:
- layer_out: bfloat16 [2048, 5120], P('dp', 'mp')
- query_grad: bfloat16 [2048, 2048], P('dp', 'mp')
- key_grad: bfloat16 [2048, 512], P('dp', 'mp')
- value_grad: bfloat16 [2048, 512], P('dp', 'mp')
- weight_grad: float32 [2048, 5120], P('mp', 'dp')
Inputs may be any that keep to these rules, and one draw needn't show every extreme that they name: `doc_lengths`: each row holds 8 lengths of 1 or more that sum to 256.
All inputs are finite; a program needn't handle non-finite values.
Results may differ from a plain program's by a relative error of at most 0.014.
Values may be sent and summed in bfloat16 or wider, within the bound.
A program may use at most 64 MiB of HBM per device.

v0:
```python
import jax
import jax.numpy as jnp
from jax import lax
from jax.sharding import PartitionSpec as P

HEAD_WIDTH = 128
TILE = 128


def local_segments(lengths, row_count):
    segment_ends = jnp.cumsum(lengths)
    positions = jnp.arange(row_count, dtype=jnp.int32)
    return jnp.sum((positions[:, None] >= segment_ends[None, :]).astype(jnp.int32), axis=1)


def to_heads(matrix):
    return matrix.reshape(matrix.shape[0], matrix.shape[1] // HEAD_WIDTH, HEAD_WIDTH).transpose(
        1, 0, 2
    )


def from_heads(tensor):
    return tensor.transpose(1, 0, 2).reshape(tensor.shape[1], tensor.shape[0] * tensor.shape[2])


def attend(queries, key_rows, value_matrix, upstreams, segment):
    head_count, row_count, head_size = queries.shape
    tile_rows = min(TILE, row_count)
    block_count = row_count // tile_rows
    softmax_scale = HEAD_WIDTH ** (-0.5)
    offsets = jnp.arange(tile_rows, dtype=jnp.int32)
    empty_rows = jnp.zeros((tile_rows, head_size), jnp.float32)
    key_sums = [empty_rows] * block_count
    value_sums = [empty_rows] * block_count
    attended_blocks = []
    grad_blocks = []
    for block_index in range(block_count):
        row_start = block_index * tile_rows
        query_tile = queries[:, row_start : row_start + tile_rows]
        upstream_tile = upstreams[:, row_start : row_start + tile_rows]
        query_segment = segment[row_start : row_start + tile_rows]
        active = [
            segment[(column_index + 1) * tile_rows - 1] >= query_segment[0]
            for column_index in range(block_index + 1)
        ]
        score_tiles = []
        for column_index in range(block_index + 1):
            column_start = column_index * tile_rows
            key_tile = key_rows[column_start : column_start + tile_rows]
            key_segment = segment[column_start : column_start + tile_rows]
            allowed = (query_segment[:, None] == key_segment[None, :]) & (
                (row_start + offsets)[:, None] >= (column_start + offsets)[None, :]
            )

            def score_tile(query_tile=query_tile, key_tile=key_tile, allowed=allowed):
                logits = (
                    jnp.einsum(
                        "hid,jd->hij", query_tile, key_tile, preferred_element_type=jnp.float32
                    )
                    * softmax_scale
                )
                return jnp.where(allowed[None], logits, -jnp.inf)

            def masked_tile():
                return jnp.full((head_count, tile_rows, tile_rows), -jnp.inf, jnp.float32)

            score_tiles.append(lax.cond(active[column_index], score_tile, masked_tile))
        logits = jnp.concatenate(score_tiles, axis=-1)
        row_max = jnp.max(logits, axis=-1, keepdims=True)
        exp_terms = jnp.exp(logits - row_max)
        probability = exp_terms / jnp.sum(exp_terms, axis=-1, keepdims=True)
        weights = probability.astype(jnp.bfloat16)
        attended = jnp.zeros((head_count, tile_rows, head_size), jnp.float32)
        grad_tiles = []
        for column_index in range(block_index + 1):
            column_start = column_index * tile_rows
            value_tile = value_matrix[column_start : column_start + tile_rows]
            weight_tile = weights[:, :, column_start : column_start + tile_rows]

            def forward_tile(
                weight_tile=weight_tile, value_tile=value_tile, upstream_tile=upstream_tile
            ):
                return (
                    jnp.einsum(
                        "hij,jd->hid", weight_tile, value_tile, preferred_element_type=jnp.float32
                    ),
                    jnp.einsum(
                        "hid,jd->hij", upstream_tile, value_tile, preferred_element_type=jnp.float32
                    ),
                )

            def empty_pair():
                return (
                    jnp.zeros((head_count, tile_rows, head_size), jnp.float32),
                    jnp.zeros((head_count, tile_rows, tile_rows), jnp.float32),
                )

            contribution, prob_grad_tile = lax.cond(active[column_index], forward_tile, empty_pair)
            attended = attended + contribution
            grad_tiles.append(prob_grad_tile)
        prob_grad = jnp.concatenate(grad_tiles, axis=-1)
        row_delta = jnp.sum(probability * prob_grad, axis=-1, keepdims=True)
        score_grad = (probability * (prob_grad - row_delta) * softmax_scale).astype(jnp.bfloat16)
        query_sum = jnp.zeros((head_count, tile_rows, head_size), jnp.float32)
        for column_index in range(block_index + 1):
            column_start = column_index * tile_rows
            key_tile = key_rows[column_start : column_start + tile_rows]
            score_piece = score_grad[:, :, column_start : column_start + tile_rows]
            weight_tile = weights[:, :, column_start : column_start + tile_rows]

            def backward_tile(
                score_piece=score_piece,
                key_tile=key_tile,
                weight_tile=weight_tile,
                query_tile=query_tile,
                upstream_tile=upstream_tile,
            ):
                return (
                    jnp.einsum(
                        "hij,jd->hid", score_piece, key_tile, preferred_element_type=jnp.float32
                    ),
                    jnp.einsum(
                        "hij,hid->jd", score_piece, query_tile, preferred_element_type=jnp.float32
                    ),
                    jnp.einsum(
                        "hij,hid->jd",
                        weight_tile,
                        upstream_tile,
                        preferred_element_type=jnp.float32,
                    ),
                )

            def empty_triple():
                return (
                    jnp.zeros((head_count, tile_rows, head_size), jnp.float32),
                    empty_rows,
                    empty_rows,
                )

            query_part, key_part, value_part = lax.cond(
                active[column_index], backward_tile, empty_triple
            )
            query_sum = query_sum + query_part
            key_sums[column_index] = key_sums[column_index] + key_part
            value_sums[column_index] = value_sums[column_index] + value_part
        attended_blocks.append(attended.astype(jnp.bfloat16))
        grad_blocks.append(query_sum.astype(jnp.bfloat16))
    return (
        jnp.concatenate(attended_blocks, axis=1),
        jnp.concatenate(grad_blocks, axis=1),
        jnp.concatenate(key_sums, axis=0),
        jnp.concatenate(value_sums, axis=0),
    )


def grad_term(grad_full, attended_heads):
    attended_flat = from_heads(attended_heads)
    return lax.dot_general(
        grad_full, attended_flat, (((0,), (0,)), ((), ())), preferred_element_type=jnp.float32
    )


def per_device(query_rows, key_rows, value_matrix, out_weight, out_grad, doc_lengths):
    row_count = query_rows.shape[0]
    weight_full = lax.all_gather(out_weight, "dp", axis=1, tiled=True)
    grad_full = lax.all_gather(out_grad, "mp", axis=1, tiled=True)
    attn_grad = lax.dot_general(
        grad_full, weight_full, (((1,), (1,)), ((), ())), preferred_element_type=jnp.float32
    ).astype(jnp.bfloat16)
    segment = local_segments(doc_lengths[0], row_count)
    queries = to_heads(query_rows)
    upstreams = to_heads(attn_grad)
    attended, query_grad, key_sum, value_sum = attend(
        queries, key_rows, value_matrix, upstreams, segment
    )
    key_grad = key_sum.astype(jnp.bfloat16)
    value_grad = value_sum.astype(jnp.bfloat16)
    weight_part = lax.psum_scatter(
        grad_term(grad_full, attended), "dp", scatter_dimension=0, tiled=True
    )
    attended_flat = from_heads(attended)
    query_grad = from_heads(query_grad)
    partial_sum = jnp.dot(attended_flat, weight_full, preferred_element_type=jnp.float32).astype(
        jnp.bfloat16
    )
    layer_out = lax.psum_scatter(
        lax.optimization_barrier(partial_sum).astype(jnp.float32).astype(jnp.bfloat16),
        "mp",
        scatter_dimension=1,
        tiled=True,
    )
    return (layer_out, query_grad, key_grad, value_grad, weight_part.T)


def solution(mesh):
    placed = (
        P("dp", "mp"),
        P("dp", "mp"),
        P("dp", "mp"),
        P("mp", "dp"),
        P("dp", "mp"),
        P("dp", None),
    )
    return jax.shard_map(
        per_device,
        mesh=mesh,
        in_specs=placed,
        out_specs=(P("dp", "mp"), P("dp", "mp"), P("dp", "mp"), P("dp", "mp"), P("mp", "dp")),
        check_vma=False,
    )
```

profile of v0, /device:TPU:27, one launch (start us, length us, event | category | flops | bytes accessed | tf_op | source)
XLA Modules:
  0.0 358.5 jit_solution(16352649762198647661)
XLA Ops:
  12.8 1.1 copy.61
  13.9 1.4 fusion.66
  15.4 1.1 conditional.9
  15.5 1.0 fusion
  16.9 1.1 conditional.11
  17.0 1.0 fusion.5
  19.6 1.1 conditional.12
  19.7 1.0 fusion.7
  21.0 1.0 fusion.61
  22.8 13.7 %all-gather.3.cloned.1.call-done = bf16[256,5120]{1,0:T(8,128)(2,1)} async-done(((bf16[256,1280]{1,0:T(8,128)(2,1)}), bf16[256,5120]{1,0:T(8,128)(2,1)}) %all-gather.3.cloned.1.call-update) | async-done | bytes 2621456 | tf_op jit(solution)/shard_map/all_gather | solution.py:166
  36.5 85.1 %all-gather.5.cloned.1.call-done = bf16[512,5120]{1,0:T(8,128)(2,1)} async-done(((bf16[512,640]{1,0:T(8,128)(2,1)}), bf16[512,5120]{1,0:T(8,128)(2,1)}) %all-gather.5.cloned.1.call-update) | async-done | bytes 5242896 | tf_op jit(solution)/shard_map/all_gather | solution.py:165
  121.6 4.8 %fusion.41 = bf16[32,4,8,128]{3,2,1,0:T(8,128)(2,1)S(1)} fusion(bf16[256,5120]{1,0:T(8,128)(2,1)} %all-gather.3.cloned.1.call-done, bf16[512,5120]{1,0:T(8,128)(2,1)} %all-gather.5.cloned.1.call-done), kind=kOutput, calls=%fused_computation.59 | convolution fusion | flops 1342308352 | bytes 8126464 | tf_op jit(solution)/shard_map/dot_general | solution.py:167
  127.1 1.4 conditional.10
  127.5 1.1 fusion.3
  130.2 5.8 %convolution_convert_fusion.2 = bf16[256,5120]{1,0:T(8,128)(2,1)} fusion(bf16[256,512]{0,1:T(8,128)(2,1)S(1)} %bitcast.105, bf16[512,5120]{1,0:T(8,128)(2,1)} %all-gather.5.cloned.1.call-done), kind=kOutput, calls=%fused_computation.49 | convolution fusion | flops 1343488000 | bytes 8126464 | tf_op jit(solution)/shard_map/dot_general | solution.py:183
  136.0 5.5 %convolution_bitcast_fusion.6 = f32[5120,512]{0,1:T(8,128)} fusion(bf16[256,512]{0,1:T(8,128)(2,1)S(1)} %bitcast.106, bf16[256,5120]{1,0:T(8,128)(2,1)S(1)} %copy-done), kind=kOutput, calls=%fused_computation.48 | convolution fusion | flops 1342177280 | bytes 13369344 | tf_op jit(solution)/shard_map/dot_general | solution.py:158
  143.0 2.3 conditional.15
  143.1 1.1 convolution_bitcast_fusion
  144.4 1.0 convolution_convert_fusion.1
  145.3 1.5 conditional.17
  146.9 1.5 conditional.16
  147.4 0.9 fusion.21
  150.4 20.8 %reduce-scatter.3.cloned.1.call-done = bf16[256,1280]{1,0:T(8,128)(2,1)} async-done(((bf16[256,5120]{1,0:T(8,128)(2,1)}), bf16[256,1280]{1,0:T(8,128)(2,1)}) %reduce-scatter.3.cloned.1.call-update) | async-done | bytes 655376 | tf_op jit(solution)/shard_map/reduce_scatter | solution.py:186
  171.3 180.7 %reduce-scatter.5.cloned.1.call-done = f32[640,512]{0,1:T(8,128)} async-done(((f32[5120,512]{0,1:T(8,128)}), f32[640,512]{0,1:T(8,128)}) %reduce-scatter.5.cloned.1.call-update) | async-done | bytes 1310736 | tf_op jit(solution)/shard_map/reduce_scatter | solution.py:178
  (87 shorter events, 14.2 us)
Async XLA Ops:
  7.2 13.8 %copy-start.11 = (bf16[256,128]{1,0:T(8,128)(2,1)S(1)}, bf16[256,128]{1,0:T(8,128)(2,1)}, u32[]{:S(2)}) copy-start(bf16[256,128]{1,0:T(8,128)(2,1)} %param.26) | copy-start | bytes 196612
  7.2 29.3 %all-gather.3.cloned.1.call-start = ((), (), s32[]{:S(2)}) async-start(), calls=%async_computation.2 | async-start | bytes 3276800 | tf_op jit(solution)/shard_map/all_gather | solution.py:166
  7.9 113.7 %all-gather.5.cloned.1.call-start = ((), (), s32[]{:S(2)}) async-start(), calls=%async_computation.3 | async-start | bytes 5898240 | tf_op jit(solution)/shard_map/all_gather | solution.py:165
  8.7 162.6 %reduce-scatter.3.cloned.1.call-start = ((), (), s32[]{:S(2)}) async-start(), calls=%async_computation.4 | async-start | bytes 3276800 | tf_op jit(solution)/shard_map/reduce_scatter | solution.py:186
  22.8 104.4 %copy-start.8 = (bf16[4,128,128]{1,2,0:T(8,128)(2,1)}, bf16[4,128,128]{1,2,0:T(8,128)(2,1)S(1)}, u32[]{:S(2)}) copy-start(bf16[4,128,128]{1,2,0:T(8,128)(2,1)S(1)} %get-tuple-element.325) | copy-start | bytes 393220
  128.6 1.0 copy-start.1
  129.0 0.7 copy-start.3
  129.5 0.7 copy-start.5
  130.2 5.8 %copy-start = (bf16[256,5120]{1,0:T(8,128)(2,1)S(1)}, bf16[256,5120]{1,0:T(8,128)(2,1)}, u32[]{:S(2)}) copy-start(bf16[256,5120]{1,0:T(8,128)(2,1)} %all-gather.3.cloned.1.call-done) | copy-start | bytes 7864324
  136.0 216.0 %reduce-scatter.5.cloned.1.call-start = ((), (), s32[]{:S(2)}) async-start(), calls=%async_computation.5 | async-start | bytes 11796480 | tf_op jit(solution)/shard_map/reduce_scatter | solution.py:178
  141.6 0.9 copy-start.4
  141.6 1.0 copy-start.6
  141.6 1.2 copy-start.7
  141.6 1.4 copy-start.2
  141.6 1.4 copy-start.10
  141.6 1.4 copy-start.9
Sparse Core Ops, SparseCore 0:
  9.5 26.8 all-gather.2
  38.7 82.8 all-gather.4
  136.1 35.0 reduce-scatter.2
  175.3 176.6 reduce-scatter.4
where the time goes:
time: 363 us; the launch traced here: 359 us
  waiting for transfers between devices  302 us (83%)
  matrix products  26 us (7%)
  between operations  18 us (5%)
  local copies, waits for them, and re-layouts  6.55 us (2%)
  other arithmetic  5.72 us (2%)
    reduce_scatter x1, waiting for transfers between devices, per_device(): lax.psum_scatter(grad_term(grad_full, attended), 'dp', scatter_dimension=...  181 us
    all_gather x1, waiting for transfers between devices, per_device(): weight_full = lax.all_gather(out_weight, 'dp', axis=1, tiled=True)  85.1 us
    reduce_scatter x1, waiting for transfers between devices, per_device(): lax.psum_scatter(lax.optimization_barrier(partial_sum).astype(jnp.float32...  20.8 us
    all_gather x1, waiting for transfers between devices, per_device(): grad_full = lax.all_gather(out_grad, 'mp', axis=1, tiled=True)  13.7 us
  transfers between devices with their start and end apart: 4, of which 4 were waited for; matrix products, arithmetic and copies ran while one was open for 6% of the time, Pallas kernels for 0%

commit v1 on v0

--- a/solution.py
+++ b/solution.py
@@ -1,6 +1,10 @@
+import functools
+
 import jax
 import jax.numpy as jnp
 from jax import lax
+from jax.experimental import pallas as pl
+from jax.experimental.pallas import tpu as pltpu
 from jax.sharding import PartitionSpec as P
 
 HEAD_WIDTH = 128
@@ -192,6 +196,399 @@
     return (layer_out, query_grad, key_grad, value_grad, weight_part.T)
 
 
+def dot(a, b, dims):
+    return lax.dot_general(a, b, (dims, ((), ())), preferred_element_type=jnp.float32)
+
+
+NN = ((1,), (0,))
+NT = ((1,), (1,))
+TN = ((0,), (0,))
+
+
+def allowed_pairs(lengths_ref, rows):
+    row_at = lax.broadcasted_iota(jnp.int32, (rows, 1), 0)
+    column_at = lax.broadcasted_iota(jnp.int32, (1, rows), 1)
+    row_segment = jnp.zeros((rows, 1), jnp.int32)
+    column_segment = jnp.zeros((1, rows), jnp.int32)
+    end = jnp.int32(0)
+    for index in range(lengths_ref.shape[1]):
+        end = end + lengths_ref[0, index]
+        row_segment = row_segment + jnp.where(row_at >= end, 1, 0)
+        column_segment = column_segment + jnp.where(column_at >= end, 1, 0)
+    return (row_segment == column_segment) & (row_at >= column_at)
+
+
+def branch_kernel(
+    n_dp,
+    n_mp,
+    lengths_ref,
+    query_ref,
+    key_ref,
+    value_ref,
+    weight_ref,
+    grad_ref,
+    layer_ref,
+    query_grad_ref,
+    key_grad_ref,
+    value_grad_ref,
+    weight_grad_ref,
+    grads,
+    heads_all,
+    upstream_part,
+    upstream_in,
+    layer_part,
+    layer_in,
+    layer_sum,
+    layer_done,
+    probs,
+    swap_send,
+    grad_send,
+    grad_recv,
+    heads_send,
+    heads_recv,
+    up_send,
+    up_recv,
+    part_send,
+    part_recv,
+    done_send,
+    done_recv,
+):
+    d = lax.axis_index("dp")
+    m = lax.axis_index("mp")
+    ratio = n_dp // n_mp
+    rows = query_ref.shape[0]
+    columns = weight_ref.shape[1]
+    head_count = query_ref.shape[1] // HEAD_WIDTH
+    group_size = query_ref.shape[1] // key_ref.shape[1]
+    scale = HEAD_WIDTH ** (-0.5)
+    home = lax.div(d, ratio)
+    slot = lax.rem(d, ratio)
+
+    def remote(source, target, send, recv, dp, mp):
+        return pltpu.make_async_remote_copy(
+            src_ref=source,
+            dst_ref=target,
+            send_sem=send,
+            recv_sem=recv,
+            device_id={"dp": dp, "mp": mp},
+            device_id_type=pl.DeviceIdType.MESH,
+        )
+
+    def swap(j):
+        return remote(
+            grad_ref.at[:, pl.ds(j * columns, columns)],
+            grads.at[d],
+            swap_send.at[j],
+            grad_recv.at[d],
+            ratio * m + j,
+            home,
+        )
+
+    def swap_here(j):
+        return pltpu.make_async_copy(
+            grad_ref.at[:, pl.ds(j * columns, columns)], grads.at[d], grad_recv.at[d]
+        )
+
+    def stays(j):
+        return (home == m) & (slot == j)
+
+    for j in range(ratio):
+        @pl.when(jnp.logical_not(stays(j)))
+        def _(j=j):
+            swap(j).start()
+
+        @pl.when(stays(j))
+        def _(j=j):
+            swap_here(j).start()
+
+    allowed = allowed_pairs(lengths_ref, rows)
+    for h in range(head_count):
+        kv = h // group_size
+        head = slice(h * HEAD_WIDTH, (h + 1) * HEAD_WIDTH)
+        kv_head = slice(kv * HEAD_WIDTH, (kv + 1) * HEAD_WIDTH)
+        logits = dot(query_ref[:, head], key_ref[:, kv_head], NT) * scale
+        logits = jnp.where(allowed, logits, -jnp.inf)
+        exp_terms = jnp.exp(logits - jnp.max(logits, axis=1, keepdims=True))
+        probability = exp_terms / jnp.sum(exp_terms, axis=1, keepdims=True)
+        probs[h] = probability
+        heads_all[d, :, head] = dot(
+            probability.astype(jnp.bfloat16), value_ref[:, kv_head], NN
+        ).astype(jnp.bfloat16)
+
+    def heads_copy(step):
+        return remote(
+            heads_all.at[d],
+            heads_all.at[d],
+            heads_send.at[step],
+            heads_recv.at[d],
+            lax.rem(d + step, n_dp),
+            m,
+        )
+
+    def grad_copy(j, step):
+        block = ratio * m + j
+        return remote(
+            grads.at[block],
+            grads.at[block],
+            grad_send.at[j, step],
+            grad_recv.at[block],
+            d,
+            lax.rem(m + step, n_mp),
+        )
+
+    def grad_arrival(block):
+        return remote(
+            grads.at[block], grads.at[block], swap_send.at[0], grad_recv.at[block], d, m
+        )
+
+    def heads_arrival(block):
+        return remote(
+            heads_all.at[block], heads_all.at[block], swap_send.at[0], heads_recv.at[block], d, m
+        )
+
+    for step in range(1, n_dp):
+        heads_copy(step).start()
+    for j in range(ratio):
+        grad_arrival(ratio * m + j).wait_recv()
+        for step in range(1, n_mp):
+            grad_copy(j, step).start()
+
+    def up_copy(block):
+        return remote(
+            upstream_part.at[block],
+            upstream_in.at[d],
+            up_send.at[block],
+            up_recv.at[d],
+            block,
+            m,
+        )
+
+    def up_step(index, carry):
+        block = lax.rem(ratio * m + index, n_dp)
+
+        @pl.when(index >= ratio)
+        def _():
+            grad_arrival(block).wait_recv()
+
+        partial = dot(grads[block], weight_ref[...], NT).astype(jnp.bfloat16)
+
+        @pl.when(block == d)
+        def _():
+            upstream_in[d] = partial
+
+        @pl.when(block != d)
+        def _():
+            upstream_part[block] = partial
+            up_copy(block).start()
+
+        return carry
+
+    lax.fori_loop(0, n_dp, up_step, 0)
+
+    def part_copy(block):
+        return remote(
+            layer_part.at[block],
+            layer_in.at[m, lax.rem(block, ratio)],
+            part_send.at[block],
+            part_recv.at[m, lax.rem(block, ratio)],
+            d,
+            lax.div(block, ratio),
+        )
+
+    def part_step(index, carry):
+        block = lax.rem(d + index, n_dp)
+
+        @pl.when(index >= 1)
+        def _():
+            heads_arrival(block).wait_recv()
+
+        partial = dot(heads_all[block], weight_ref[...], NN).astype(jnp.bfloat16)
+
+        @pl.when(lax.div(block, ratio) == m)
+        def _():
+            layer_in[m, lax.rem(block, ratio)] = partial
+
+        @pl.when(lax.div(block, ratio) != m)
+        def _():
+            layer_part[block] = partial
+            part_copy(block).start()
+
+        return carry
+
+    lax.fori_loop(0, n_dp, part_step, 0)
+
+    weight_grad_ref[...] = jnp.zeros_like(weight_grad_ref)
+
+    def weight_step(block, carry):
+        weight_grad_ref[...] += dot(heads_all[block], grads[block], TN)
+        return carry
+
+    lax.fori_loop(0, n_dp, weight_step, 0)
+
+    def part_arrival(source, j):
+        return remote(
+            layer_in.at[source, j],
+            layer_in.at[source, j],
+            swap_send.at[0],
+            part_recv.at[source, j],
+            d,
+            m,
+        )
+
+    def done_copy(j):
+        return remote(
+            layer_sum.at[j],
+            layer_done.at[slot],
+            done_send.at[j],
+            done_recv.at[slot],
+            ratio * m + j,
+            home,
+        )
+
+    for j in range(ratio):
+        for step in range(1, n_mp):
+            part_arrival(lax.rem(m + step, n_mp), j).wait_recv()
+        total = layer_in[0, j].astype(jnp.float32)
+        for source in range(1, n_mp):
+            total = total + layer_in[source, j].astype(jnp.float32)
+        layer_sum[j] = total.astype(jnp.bfloat16)
+
+        @pl.when(jnp.logical_not(stays(j)))
+        def _(j=j):
+            done_copy(j).start()
+
+        @pl.when(stays(j))
+        def _(j=j):
+            layer_done[j] = layer_sum[j]
+
+    def up_arrival(block):
+        return remote(
+            upstream_in.at[block], upstream_in.at[block], swap_send.at[0], up_recv.at[block], d, m
+        )
+
+    for step in range(1, n_dp):
+        up_arrival(lax.rem(d + step, n_dp)).wait_recv()
+    for h in range(head_count):
+        kv = h // group_size
+        head = slice(h * HEAD_WIDTH, (h + 1) * HEAD_WIDTH)
+        kv_head = slice(kv * HEAD_WIDTH, (kv + 1) * HEAD_WIDTH)
+        upstream = upstream_in[0, :, head].astype(jnp.float32)
+        for block in range(1, n_dp):
+            upstream = upstream + upstream_in[block, :, head].astype(jnp.float32)
+        upstream = upstream.astype(jnp.bfloat16)
+        probability = probs[h]
+        prob_grad = dot(upstream, value_ref[:, kv_head], NT)
+        row_delta = jnp.sum(probability * prob_grad, axis=1, keepdims=True)
+        score_grad = (probability * (prob_grad - row_delta) * scale).astype(jnp.bfloat16)
+        query_grad_ref[:, head] = dot(score_grad, key_ref[:, kv_head], NN).astype(jnp.bfloat16)
+        key_term = dot(score_grad, query_ref[:, head], TN)
+        value_term = dot(probability.astype(jnp.bfloat16), upstream, TN)
+        if h % group_size == 0:
+            key_sum, value_sum = key_term, value_term
+        else:
+            key_sum, value_sum = key_sum + key_term, value_sum + value_term
+        if h % group_size == group_size - 1:
+            key_grad_ref[:, kv_head] = key_sum.astype(jnp.bfloat16)
+            value_grad_ref[:, kv_head] = value_sum.astype(jnp.bfloat16)
+
+    for j in range(ratio):
+        @pl.when(jnp.logical_not(stays(j)))
+        def _(j=j):
+            remote(
+                layer_done.at[j], layer_done.at[j], swap_send.at[0], done_recv.at[j], d, m
+            ).wait_recv()
+
+        layer_ref[:, j * columns : (j + 1) * columns] = layer_done[j]
+
+    for j in range(ratio):
+        @pl.when(jnp.logical_not(stays(j)))
+        def _(j=j):
+            swap(j).wait_send()
+            done_copy(j).wait_send()
+
+        for step in range(1, n_mp):
+            grad_copy(j, step).wait_send()
+    for step in range(1, n_dp):
+        heads_copy(step).wait_send()
+
+    def drain_step(block, carry):
+        @pl.when(block != d)
+        def _():
+            up_copy(block).wait_send()
+
+        @pl.when(lax.div(block, ratio) != m)
+        def _():
+            part_copy(block).wait_send()
+
+        return carry
+
+    lax.fori_loop(0, n_dp, drain_step, 0)
+
+
+def fused(n_dp, n_mp, query_rows, key_rows, value_matrix, out_weight, out_grad, doc_lengths):
+    rows, width = query_rows.shape
+    columns = out_weight.shape[1]
+    ratio = n_dp // n_mp
+    vmem = pl.BlockSpec(memory_space=pltpu.VMEM)
+    dma = pltpu.SemaphoreType.DMA
+    return pl.pallas_call(
+        functools.partial(branch_kernel, n_dp, n_mp),
+        out_shape=(
+            jax.ShapeDtypeStruct(out_grad.shape, jnp.bfloat16),
+            jax.ShapeDtypeStruct(query_rows.shape, jnp.bfloat16),
+            jax.ShapeDtypeStruct(key_rows.shape, jnp.bfloat16),
+            jax.ShapeDtypeStruct(value_matrix.shape, jnp.bfloat16),
+            jax.ShapeDtypeStruct(out_weight.shape, jnp.float32),
+        ),
+        in_specs=[pl.BlockSpec(memory_space=pltpu.SMEM)] + [vmem] * 5,
+        out_specs=(vmem,) * 5,
+        scratch_shapes=[
+            pltpu.VMEM((n_dp, rows, columns), jnp.bfloat16),
+            pltpu.VMEM((n_dp, rows, width), jnp.bfloat16),
+            pltpu.VMEM((n_dp, rows, width), jnp.bfloat16),
+            pltpu.VMEM((n_dp, rows, width), jnp.bfloat16),
+            pltpu.VMEM((n_dp, rows, columns), jnp.bfloat16),
+            pltpu.VMEM((n_mp, ratio, rows, columns), jnp.bfloat16),
+            pltpu.VMEM((ratio, rows, columns), jnp.bfloat16),
+            pltpu.VMEM((ratio, rows, columns), jnp.bfloat16),
+            pltpu.VMEM((width // HEAD_WIDTH, rows, rows), jnp.float32),
+            dma((ratio,)),
+            dma((ratio, n_mp)),
+            dma((n_dp,)),
+            dma((n_dp,)),
+            dma((n_dp,)),
+            dma((n_dp,)),
+            dma((n_dp,)),
+            dma((n_dp,)),
+            dma((n_mp, ratio)),
+            dma((ratio,)),
+            dma((ratio,)),
+        ],
+        compiler_params=pltpu.CompilerParams(
+            has_side_effects=True, vmem_limit_bytes=56 * 1024 * 1024
+        ),
+    )(doc_lengths, query_rows, key_rows, value_matrix, out_weight, out_grad)
+
+
+def body_of(n_dp, n_mp):
+    def body(query_rows, key_rows, value_matrix, out_weight, out_grad, doc_lengths):
+        arrays = (query_rows, key_rows, value_matrix, out_weight, out_grad, doc_lengths)
+        columns = out_weight.shape[1]
+        rows, width = query_rows.shape
+        held = 2 * n_dp * rows * (4 * columns + 3 * width)
+        if (
+            columns % 128 == 0
+            and rows % 128 == 0
+            and n_dp % n_mp == 0
+            and columns * (n_dp // n_mp) == out_grad.shape[1]
+            and held < 24 * 1024 * 1024
+        ):
+            return fused(n_dp, n_mp, *arrays)
+        return per_device(*arrays)
+
+    return body
+
+
 def solution(mesh):
     placed = (
         P("dp", "mp"),
@@ -202,7 +599,7 @@
         P("dp", None),
     )
     return jax.shard_map(
-        per_device,
+        body_of(mesh.shape["dp"], mesh.shape["mp"]),
         mesh=mesh,
         in_specs=placed,
         out_specs=(P("dp", "mp"), P("dp", "mp"), P("dp", "mp"), P("dp", "mp"), P("mp", "dp")),

time: 363 us -> 171 us (0.47); the launches traced: 359 us -> 171 us
  waiting for transfers between devices: 302 us -> 0 us
  Pallas kernels: 0 us -> 164 us
  matrix products: 26 us -> 0 us
  between operations: 18 us -> 0.67 us
  other arithmetic: 5.72 us -> 0 us
    reduce_scatter x2 -> x0, waiting for transfers between devices: 202 us -> none  [the longest x1 181 us: per_device(): lax.psum_scatter(grad_term(grad_full, attended), 'dp', scatter_dimension=...]
    pallas_call x0 -> x1, Pallas kernels: none -> 164 us  [fused(): pl.pallas_call(functools.partial(branch_kernel, n_dp, n_mp), out_shape=(j...]
    all_gather x2 -> x0, waiting for transfers between devices: 98.8 us -> none  [the longest x1 85.1 us: per_device(): weight_full = lax.all_gather(out_weight, 'dp', axis=1, tiled=True)]
    dot_general x16 -> x0, matrix products: 24.1 us -> none  [the longest x1 5.75 us: per_device(): jnp.dot(attended_flat, weight_full, preferred_element_type=jnp.float32)]
  transfers between devices with their start and end apart: 4 -> 0, of which waited for: 4 -> 0; matrix products, arithmetic and copies ran while one was open for 6% -> 0% of each run, Pallas kernels for 0% -> 0%
where the time goes in v1:
time: 171 us
  Pallas kernels  164 us (96%)
  local copies, waits for them, and re-layouts  6.07 us (4%)
    pallas_call x1, Pallas kernels, fused(): pl.pallas_call(functools.partial(branch_kernel, n_dp, n_mp), out_shape=(j...  164 us
    unnamed x11, local copies, waits for them, and re-layouts  6.07 us

profile of v1, /device:TPU:27, one launch (start us, length us, event | category | flops | bytes accessed | tf_op | source)
XLA Modules:
  0.0 170.6 jit_solution(521864653676612190)
XLA Ops:
  0.6 163.9 %shard_map.101 = (bf16[256,1280]{1,0:T(8,128)(2,1)}, bf16[256,512]{1,0:T(8,128)(2,1)}, bf16[256,128]{1,0:T(8,128)(2,1)}, bf16[256,128]{1,0:T(8,128)(2,1)}, f32[512,640]{1,0:T(8,128)}) custom-call(s32[1,8]{1,0:T(1,128)} %lengths_ref.1, bf16[256,512]{1,0:T(8,128)(2,1)} %query_ref.1, bf16[256,128]{1,0:T(8,128)(2,1)} %key_ref.1, bf16[256,128]{1,0:T(8,128)(2,1)} %value_ref.1, ...), custom_call_target="tpu_custom_call" | custom-call | tf_op jit(solution)/shard_map/pallas_call | solution.py:534
  164.5 0.0 copy-start.2
  164.6 0.0 copy-start.1
  164.6 0.0 copy-start
  164.6 2.1 %copy.16 = bf16[256,1280]{1,0:T(8,128)(2,1)} copy(bf16[256,1280]{1,0:T(8,128)(2,1)} %get-tuple-element.10) | data formatting | bytes 1310720
  166.6 1.7 copy.17
  168.3 0.0 copy-done.2
  168.3 0.6 copy.18
  168.9 0.0 copy-done.1
  169.0 0.6 copy.19
  169.6 0.0 copy-done
  169.6 1.1 copy.20
Async XLA Ops:
  164.5 3.8 %copy-start.2 = (bf16[256,128]{1,0:T(8,128)(2,1)S(1)}, bf16[256,128]{1,0:T(8,128)(2,1)}, u32[]{:S(2)}) copy-start(bf16[256,128]{1,0:T(8,128)(2,1)} %get-tuple-element.12) | copy-start | bytes 196612
  164.6 4.4 %copy-start.1 = (bf16[256,128]{1,0:T(8,128)(2,1)S(1)}, bf16[256,128]{1,0:T(8,128)(2,1)}, u32[]{:S(2)}) copy-start(bf16[256,128]{1,0:T(8,128)(2,1)} %get-tuple-element.13) | copy-start | bytes 196612
  164.6 5.0 %copy-start = (f32[512,640]{1,0:T(8,128)S(1)}, f32[512,640]{1,0:T(8,128)}, u32[]{:S(2)}) copy-start(f32[512,640]{1,0:T(8,128)} %get-tuple-element.14) | copy-start | bytes 3932164

commit v2 on v1

--- a/solution.py
+++ b/solution.py
@@ -235,6 +235,8 @@
     grads,
     heads_all,
     upstream_part,
+    twin_in,
+    pair_sum,
     upstream_in,
     layer_part,
     layer_in,
@@ -247,6 +249,8 @@
     heads_send,
     heads_recv,
     up_send,
+    twin_recv,
+    pair_send,
     up_recv,
     part_send,
     part_recv,
@@ -263,6 +267,12 @@
     scale = HEAD_WIDTH ** (-0.5)
     home = lax.div(d, ratio)
     slot = lax.rem(d, ratio)
+    keeper = lax.rem(d, n_mp)
+    line = n_dp // 2
+    spot = lax.div(d, 2)
+    side = lax.rem(d, 2)
+    twin = 2 * spot + 1 - side
+    sibling = 2 * lax.div(m, 2) + 1 - lax.rem(m, 2)
 
     def remote(source, target, send, recv, dp, mp):
         return pltpu.make_async_remote_copy(
@@ -281,7 +291,7 @@
             swap_send.at[j],
             grad_recv.at[d],
             ratio * m + j,
-            home,
+            keeper,
         )
 
     def swap_here(j):
@@ -290,7 +300,10 @@
         )
 
     def stays(j):
-        return (home == m) & (slot == j)
+        return (keeper == m) & (d == ratio * m + j)
+
+    def summed_here(j):
+        return (home == m) & (d == m + n_mp * j)
 
     for j in range(ratio):
         @pl.when(jnp.logical_not(stays(j)))
@@ -315,26 +328,64 @@
             probability.astype(jnp.bfloat16), value_ref[:, kv_head], NN
         ).astype(jnp.bfloat16)
 
-    def heads_copy(step):
-        return remote(
-            heads_all.at[d],
-            heads_all.at[d],
-            heads_send.at[step],
-            heads_recv.at[d],
-            lax.rem(d + step, n_dp),
+    def heads_copy(block, way):
+        target = (d + 2, d - 2, twin)[way]
+        return remote(
+            heads_all.at[block],
+            heads_all.at[block],
+            heads_send.at[block, way],
+            heads_recv.at[block],
+            target,
             m,
         )
 
-    def grad_copy(j, step):
-        block = ratio * m + j
+    def heads_pass(distance, started):
+        def act(block, way):
+            if started:
+                heads_copy(block, way).start()
+            else:
+                heads_copy(block, way).wait_send()
+
+        for way, sign in ((0, -1), (1, 1)):
+            block = d + sign * 2 * distance
+            origin = spot + sign * distance
+            onward = spot - sign
+
+            @pl.when((origin >= 0) & (origin < line))
+            def _(block=block, way=way, onward=onward):
+                if started and distance > 0:
+                    heads_arrival(block).wait_recv()
+
+                @pl.when((onward >= 0) & (onward < line))
+                def _():
+                    act(block, way)
+
+                if distance > 0:
+                    act(block, 2)
+        if distance == 0:
+            act(d, 2)
+
+    def grad_copy(block, step, mp):
         return remote(
             grads.at[block],
             grads.at[block],
-            grad_send.at[j, step],
+            grad_send.at[lax.div(block, n_mp), step],
             grad_recv.at[block],
             d,
-            lax.rem(m + step, n_mp),
-        )
+            mp,
+        )
+
+    def own_grad(j):
+        return [grad_copy(m + n_mp * j, 0, sibling)] + [
+            grad_copy(m + n_mp * j, step, lax.rem(m + 2 * step, n_mp))
+            for step in range(1, n_mp // 2)
+        ]
+
+    def across(j, step):
+        return lax.rem(m + n_mp - 2 * step, n_mp) + n_mp * j
+
+    def passed_grad(j, step):
+        return grad_copy(across(j, step), n_mp // 2 - 1 + step, sibling)
 
     def grad_arrival(block):
         return remote(
@@ -346,76 +397,121 @@
             heads_all.at[block], heads_all.at[block], swap_send.at[0], heads_recv.at[block], d, m
         )
 
-    for step in range(1, n_dp):
-        heads_copy(step).start()
+    heads_pass(0, True)
     for j in range(ratio):
-        grad_arrival(ratio * m + j).wait_recv()
-        for step in range(1, n_mp):
-            grad_copy(j, step).start()
+        grad_arrival(m + n_mp * j).wait_recv()
+        for copy in own_grad(j):
+            copy.start()
 
     def up_copy(block):
         return remote(
             upstream_part.at[block],
-            upstream_in.at[d],
+            twin_in.at[lax.div(block, 2)],
             up_send.at[block],
-            up_recv.at[d],
-            block,
+            twin_recv.at[lax.div(block, 2)],
+            twin,
             m,
         )
 
-    def up_step(index, carry):
-        block = lax.rem(ratio * m + index, n_dp)
-
-        @pl.when(index >= ratio)
+    def up_block(block):
+        upstream_part[block] = dot(grads[block], weight_ref[...], NT).astype(jnp.bfloat16)
+
+        @pl.when(lax.rem(block, 2) != side)
         def _():
-            grad_arrival(block).wait_recv()
-
-        partial = dot(grads[block], weight_ref[...], NT).astype(jnp.bfloat16)
-
-        @pl.when(block == d)
+            up_copy(block).start()
+
+    def own_step(index, carry):
+        up_block(m + n_mp * index)
+        return carry
+
+    lax.fori_loop(0, ratio, own_step, 0)
+    for step in range(1, n_mp // 2):
+        for j in range(ratio):
+            grad_arrival(across(j, step)).wait_recv()
+            passed_grad(j, step).start()
+    heads_pass(1, True)
+
+    def near_step(index, carry):
+        up_block(lax.rem(m + n_mp - 2 * (1 + lax.div(index, ratio)), n_mp) + n_mp * lax.rem(index, ratio))
+        return carry
+
+    lax.fori_loop(0, ratio * (n_mp // 2 - 1), near_step, 0)
+
+    def far_step(index, carry):
+        block = lax.rem(sibling + n_mp - 2 * lax.div(index, ratio), n_mp) + n_mp * lax.rem(index, ratio)
+        grad_arrival(block).wait_recv()
+        up_block(block)
+        return carry
+
+    lax.fori_loop(0, ratio, far_step, 0)
+    for distance in range(2, line):
+        heads_pass(distance, True)
+    lax.fori_loop(ratio, ratio * (n_mp // 2), far_step, 0)
+
+    def pair_copy(place):
+        return remote(
+            pair_sum.at[place],
+            upstream_in.at[spot],
+            pair_send.at[place],
+            up_recv.at[spot],
+            2 * place + side,
+            m,
+        )
+
+    def pair_step(index, carry):
+        place = lax.rem(spot + 1 + index, line)
+        remote(
+            twin_in.at[place], twin_in.at[place], swap_send.at[0], twin_recv.at[place], d, m
+        ).wait_recv()
+        total = (
+            upstream_part[2 * place + side].astype(jnp.float32)
+            + twin_in[place].astype(jnp.float32)
+        ).astype(jnp.bfloat16)
+
+        @pl.when(place == spot)
         def _():
-            upstream_in[d] = partial
-
-        @pl.when(block != d)
+            upstream_in[spot] = total
+
+        @pl.when(place != spot)
         def _():
-            upstream_part[block] = partial
-            up_copy(block).start()
+            pair_sum[place] = total
+            pair_copy(place).start()
 
         return carry
 
-    lax.fori_loop(0, n_dp, up_step, 0)
-
     def part_copy(block):
         return remote(
             layer_part.at[block],
-            layer_in.at[m, lax.rem(block, ratio)],
+            layer_in.at[m, lax.div(block, n_mp)],
             part_send.at[block],
-            part_recv.at[m, lax.rem(block, ratio)],
+            part_recv.at[m, lax.div(block, n_mp)],
             d,
-            lax.div(block, ratio),
+            lax.rem(block, n_mp),
         )
 
     def part_step(index, carry):
-        block = lax.rem(d + index, n_dp)
-
-        @pl.when(index >= 1)
+        block = lax.rem(lax.rem(d + 2 * index, n_dp) + lax.div(index, line) * (twin - d) + n_dp, n_dp)
+
+        @pl.when(index >= line)
         def _():
             heads_arrival(block).wait_recv()
 
         partial = dot(heads_all[block], weight_ref[...], NN).astype(jnp.bfloat16)
 
-        @pl.when(lax.div(block, ratio) == m)
+        @pl.when(lax.rem(block, n_mp) == m)
         def _():
-            layer_in[m, lax.rem(block, ratio)] = partial
-
-        @pl.when(lax.div(block, ratio) != m)
+            layer_in[m, lax.div(block, n_mp)] = partial
+
+        @pl.when(lax.rem(block, n_mp) != m)
         def _():
             layer_part[block] = partial
             part_copy(block).start()
 
         return carry
 
-    lax.fori_loop(0, n_dp, part_step, 0)
+    lax.fori_loop(0, line, part_step, 0)
+    lax.fori_loop(0, line, pair_step, 0)
+    lax.fori_loop(line, n_dp, part_step, 0)
 
     weight_grad_ref[...] = jnp.zeros_like(weight_grad_ref)
 
@@ -441,7 +537,7 @@
             layer_done.at[slot],
             done_send.at[j],
             done_recv.at[slot],
-            ratio * m + j,
+            m + n_mp * j,
             home,
         )
 
@@ -453,27 +549,27 @@
             total = total + layer_in[source, j].astype(jnp.float32)
         layer_sum[j] = total.astype(jnp.bfloat16)
 
-        @pl.when(jnp.logical_not(stays(j)))
+        @pl.when(jnp.logical_not(summed_here(j)))
         def _(j=j):
             done_copy(j).start()
 
-        @pl.when(stays(j))
+        @pl.when(summed_here(j))
         def _(j=j):
-            layer_done[j] = layer_sum[j]
+            layer_done[slot] = layer_sum[j]
 
     def up_arrival(block):
         return remote(
             upstream_in.at[block], upstream_in.at[block], swap_send.at[0], up_recv.at[block], d, m
         )
 
-    for step in range(1, n_dp):
-        up_arrival(lax.rem(d + step, n_dp)).wait_recv()
+    for step in range(1, line):
+        up_arrival(lax.rem(spot + step, line)).wait_recv()
     for h in range(head_count):
         kv = h // group_size
         head = slice(h * HEAD_WIDTH, (h + 1) * HEAD_WIDTH)
         kv_head = slice(kv * HEAD_WIDTH, (kv + 1) * HEAD_WIDTH)
         upstream = upstream_in[0, :, head].astype(jnp.float32)
-        for block in range(1, n_dp):
+        for block in range(1, line):
             upstream = upstream + upstream_in[block, :, head].astype(jnp.float32)
         upstream = upstream.astype(jnp.bfloat16)
         probability = probs[h]
@@ -504,19 +600,26 @@
         @pl.when(jnp.logical_not(stays(j)))
         def _(j=j):
             swap(j).wait_send()
+
+        @pl.when(jnp.logical_not(summed_here(j)))
+        def _(j=j):
             done_copy(j).wait_send()
 
-        for step in range(1, n_mp):
-            grad_copy(j, step).wait_send()
-    for step in range(1, n_dp):
-        heads_copy(step).wait_send()
+        for copy in own_grad(j):
+            copy.wait_send()
+        for step in range(1, n_mp // 2):
+            passed_grad(j, step).wait_send()
+    for distance in range(line):
+        heads_pass(distance, False)
+    for step in range(1, line):
+        pair_copy(lax.rem(spot + step, line)).wait_send()
 
     def drain_step(block, carry):
-        @pl.when(block != d)
+        @pl.when(lax.rem(block, 2) != side)
         def _():
             up_copy(block).wait_send()
 
-        @pl.when(lax.div(block, ratio) != m)
+        @pl.when(lax.rem(block, n_mp) != m)
         def _():
             part_copy(block).wait_send()
 
@@ -546,7 +649,9 @@
             pltpu.VMEM((n_dp, rows, columns), jnp.bfloat16),
             pltpu.VMEM((n_dp, rows, width), jnp.bfloat16),
             pltpu.VMEM((n_dp, rows, width), jnp.bfloat16),
-            pltpu.VMEM((n_dp, rows, width), jnp.bfloat16),
+            pltpu.VMEM((n_dp // 2, rows, width), jnp.bfloat16),
+            pltpu.VMEM((n_dp // 2, rows, width), jnp.bfloat16),
+            pltpu.VMEM((n_dp // 2, rows, width), jnp.bfloat16),
             pltpu.VMEM((n_dp, rows, columns), jnp.bfloat16),
             pltpu.VMEM((n_mp, ratio, rows, columns), jnp.bfloat16),
             pltpu.VMEM((ratio, rows, columns), jnp.bfloat16),
@@ -555,10 +660,12 @@
             dma((ratio,)),
             dma((ratio, n_mp)),
             dma((n_dp,)),
+            dma((n_dp, 3)),
             dma((n_dp,)),
             dma((n_dp,)),
-            dma((n_dp,)),
-            dma((n_dp,)),
+            dma((n_dp // 2,)),
+            dma((n_dp // 2,)),
+            dma((n_dp // 2,)),
             dma((n_dp,)),
             dma((n_mp, ratio)),
             dma((ratio,)),
@@ -580,6 +687,7 @@
             columns % 128 == 0
             and rows % 128 == 0
             and n_dp % n_mp == 0
+            and n_mp % 2 == 0
             and columns * (n_dp // n_mp) == out_grad.shape[1]
             and held < 24 * 1024 * 1024
         ):

time: 171 us -> 127 us (0.74)
  the two profiles are of different devices: /device:TPU:27 before, /device:TPU:14 now
where the time goes in v2:
time: 127 us
  Pallas kernels  120 us (94%)
  local copies, waits for them, and re-layouts  6.07 us (5%)
    pallas_call x1, Pallas kernels, fused(): pl.pallas_call(functools.partial(branch_kernel, n_dp, n_mp), out_shape=(j...  120 us
    unnamed x11, local copies, waits for them, and re-layouts  6.07 us

profile of v2, /device:TPU:14, one launch (start us, length us, event | category | flops | bytes accessed | tf_op | source)
XLA Modules:
  0.0 127.2 jit_solution(11049831392238074075)
XLA Ops:
  0.6 120.5 %shard_map.101 = (bf16[256,1280]{1,0:T(8,128)(2,1)}, bf16[256,512]{1,0:T(8,128)(2,1)}, bf16[256,128]{1,0:T(8,128)(2,1)}, bf16[256,128]{1,0:T(8,128)(2,1)}, f32[512,640]{1,0:T(8,128)}) custom-call(s32[1,8]{1,0:T(1,128)} %lengths_ref.1, bf16[256,512]{1,0:T(8,128)(2,1)} %query_ref.1, bf16[256,128]{1,0:T(8,128)(2,1)} %key_ref.1, bf16[256,128]{1,0:T(8,128)(2,1)} %value_ref.1, ...), custom_call_target="tpu_custom_call" | custom-call | tf_op jit(solution)/shard_map/pallas_call | solution.py:637
  121.1 0.0 copy-start.2
  121.1 0.0 copy-start.1
  121.1 0.0 copy-start
  121.1 2.1 %copy.16 = bf16[256,1280]{1,0:T(8,128)(2,1)} copy(bf16[256,1280]{1,0:T(8,128)(2,1)} %get-tuple-element.10) | data formatting | bytes 1310720
  123.2 1.7 %copy.17 = bf16[256,512]{1,0:T(8,128)(2,1)} copy(bf16[256,512]{1,0:T(8,128)(2,1)} %get-tuple-element.11) | data formatting | bytes 524288
  124.9 0.0 copy-done.2
  124.9 0.6 copy.18
  125.5 0.0 copy-done.1
  125.5 0.6 copy.19
  126.1 0.0 copy-done
  126.1 1.1 copy.20
Async XLA Ops:
  121.1 3.8 %copy-start.2 = (bf16[256,128]{1,0:T(8,128)(2,1)S(1)}, bf16[256,128]{1,0:T(8,128)(2,1)}, u32[]{:S(2)}) copy-start(bf16[256,128]{1,0:T(8,128)(2,1)} %get-tuple-element.12) | copy-start | bytes 196612
  121.1 4.4 %copy-start.1 = (bf16[256,128]{1,0:T(8,128)(2,1)S(1)}, bf16[256,128]{1,0:T(8,128)(2,1)}, u32[]{:S(2)}) copy-start(bf16[256,128]{1,0:T(8,128)(2,1)} %get-tuple-element.13) | copy-start | bytes 196612
  121.1 5.0 %copy-start = (f32[512,640]{1,0:T(8,128)S(1)}, f32[512,640]{1,0:T(8,128)}, u32[]{:S(2)}) copy-start(f32[512,640]{1,0:T(8,128)} %get-tuple-element.14) | copy-start | bytes 3932164
